TPU v7x, 32 devices: a whole 2x2x4 slice. The times are simulated.
32 devices in a mesh: dp: 16 (over z, y, x), rep: 2 (over core).
Axes of the slice: x: 2, y: 2, z: 4, core: 2. Of those that a mesh axis runs over, the one named last changes fastest.
Arguments:
- queries: bfloat16 [2048, 2048], P(('dp', 'rep')), may hold values from -24 to 24
- documents: bfloat16 [2048, 2048], P(('dp', 'rep')), may hold values from -24 to 24
- partner: int32 [2048], P(('dp', 'rep')), may hold values from 0 to 2047, each once
Outputs:
- grad_queries: float32 [2048, 2048], P(('dp', 'rep'))
- grad_documents: float32 [2048, 2048], P(('dp', 'rep'))
Inputs may be any that keep to these rules, and one draw needn't show every extreme that they name: `partner`: every document index appears exactly once.
All inputs are finite; a program needn't handle non-finite values.
Results may differ from a plain program's by a relative error of at most 0.0031.
Values may be sent and summed in bfloat16 or wider, within the bound.
No kernel may reach another device: no remote copies, remote signals or barrier semaphores. Data moves between devices by JAX's collectives and lax.ppermute only.
A program may use at most 256 MiB of HBM per device.

v0:
```python
import jax
import jax.numpy as jnp
from jax import lax
from jax.sharding import PartitionSpec as P

WIDTHS = 9
logit_gain = 3.0


def merged(x, axis, combine):
    everything = jax.tree.map(lambda part: lax.all_gather(part, axis), x)
    leading = jax.tree.map(lambda part: part[0], everything)

    def hop(k, so_far):
        return combine(so_far, jax.tree.map(lambda part: part[k], everything))

    return lax.fori_loop(1, lax.axis_size(axis), hop, leading)


def contract(first_op, second_op):
    return lax.dot_general(
        first_op, second_op, (((1,), (1,)), ((), ())), preferred_element_type=jnp.float32
    )


def width_list(feature_dim):
    return [feature_dim >> WIDTHS - 1 - nested for nested in range(WIDTHS)]


def scores(first_op, second_op):
    uppers = width_list(first_op.shape[1])
    result = []
    running = jnp.zeros((first_op.shape[0], second_op.shape[0]), jnp.float32)
    lower_col = 0
    for upper_col in uppers:
        running = running + contract(
            first_op[:, lower_col:upper_col], second_op[:, lower_col:upper_col]
        )
        result.append(running * (logit_gain * upper_col ** (-0.5)))
        lower_col = upper_col
    return result


def band_sums(logit_list, total_list, target, uppers):
    bands = [None] * len(uppers)
    running = None
    for nested in reversed(range(len(uppers))):
        scale = logit_gain * uppers[nested] ** (-0.5)
        weight = (jnp.exp(logit_list[nested] - total_list[nested]) - target) * scale
        running = weight if running is None else running + weight
        bands[nested] = running.astype(jnp.bfloat16)
    return bands


def spread(bands, operand, uppers):
    pieces = []
    lower_col = 0
    for nested, upper_col in enumerate(uppers):
        block_part = operand[:, lower_col:upper_col]
        product = jnp.dot(bands[nested], block_part, preferred_element_type=jnp.float32)
        pieces.append(product)
        lower_col = upper_col
    return jnp.concatenate(pieces, axis=1)


def combine(first_pair, second_pair):
    biggest = jnp.maximum(first_pair[0], second_pair[0])
    return (
        biggest,
        first_pair[1] * jnp.exp(first_pair[0] - biggest)
        + second_pair[1] * jnp.exp(second_pair[0] - biggest),
    )


def on_device(queries, documents, partner):
    own_rows = queries.shape[0]
    uppers = width_list(queries.shape[1])
    rep_index = lax.axis_index("rep")
    dp_index = lax.axis_index("dp")
    rep_count = lax.axis_size("rep")
    every_rows = None
    every_partner = None
    every_rows, every_partner = (
        lax.all_gather(queries, ("dp", "rep"), axis=0, tiled=True),
        lax.all_gather(partner, ("dp", "rep"), axis=0, tiled=True),
    )
    pair_rows, pair_partner = (
        lax.all_gather(queries, "rep", axis=0, tiled=True),
        lax.all_gather(partner, "rep", axis=0, tiled=True),
    )
    partner_docs = lax.all_gather(documents, "dp", axis=0, tiled=True)
    col_pos = jnp.arange(partner_docs.shape[0], dtype=jnp.int32)
    col_ids = (col_pos // own_rows * rep_count + rep_index) * own_rows + col_pos % own_rows
    target = (pair_partner[:, None] == col_ids[None, :]).astype(jnp.float32)
    logit_list = scores(pair_rows, partner_docs)
    row_peaks = jnp.stack([jnp.max(logits, axis=1) for logits in logit_list])
    masses = jnp.stack(
        [
            jnp.sum(jnp.exp(logits - row_peaks[nested][:, None]), axis=1)
            for nested, logits in enumerate(logit_list)
        ]
    )
    row_peaks, masses = merged((row_peaks, masses), "rep", combine)
    totals = row_peaks + jnp.log(masses)
    bands = band_sums(
        logit_list, [totals[nested][:, None] for nested in range(len(uppers))], target, uppers
    )
    partial_queries = spread(bands, partner_docs, uppers)
    grad_queries = lax.psum_scatter(partial_queries, "rep", scatter_dimension=0, tiled=True)
    all_totals = lax.all_gather(totals, "dp", axis=1, tiled=True)
    own_ids = (dp_index * rep_count + rep_index) * own_rows + jnp.arange(own_rows, dtype=jnp.int32)
    own_target = (own_ids[:, None] == every_partner[None, :]).astype(jnp.float32)
    own_logits = scores(documents, every_rows)
    own_bands = band_sums(
        own_logits,
        [all_totals[nested][None, :] for nested in range(len(uppers))],
        own_target,
        uppers,
    )
    grad_documents = spread(own_bands, every_rows, uppers)
    return (grad_queries, grad_documents)


def solution(mesh):
    return jax.shard_map(
        on_device,
        mesh=mesh,
        in_specs=(P(("dp", "rep"), None), P(("dp", "rep"), None), P(("dp", "rep"))),
        out_specs=(P(("dp", "rep"), None), P(("dp", "rep"), None)),
        check_vma=False,
    )
```

profile of v0, /device:TPU:0, one launch (start us, length us, event | category | flops | bytes accessed | tf_op | source)
XLA Modules:
  0.0 192.3 jit_solution(15431763824458192233)
XLA Ops:
  7.2 0.7 all-gather.7.cloned.1.call-update
  7.9 0.7 all-gather.9.cloned.1.call-update
  8.7 1.2 dynamic-slice
  10.6 0.9 dynamic-update-slice
  11.5 0.8 dynamic-update-slice.1
  12.3 2.0 %all-reduce = s32[128]{0:T(128)S(1)} all-reduce(s32[128]{0:T(128)S(1)} %dynamic-update-slice), channel_id=1, replica_groups=mesh['dp'=16,'rep'=2] {'rep'}, use_global_device_ids=true, to_apply=%add | all-reduce | flops 128 | bytes 1024
  14.3 42.2 %all-reduce.1 = s32[2048]{0:T(1024)S(1)} all-reduce(s32[2048]{0:T(1024)S(1)} %dynamic-update-slice.1), channel_id=1, replica_groups=mesh['dp'=16,'rep'=2] {'dp','rep'}, use_global_device_ids=true, to_apply=%add.1 | all-reduce | flops 2048 | bytes 16384
  56.5 2.4 %all_gather.30 = bf16[128,2048]{1,0:T(8,128)(2,1)S(1)} all-gather(bf16[64,2048]{1,0:T(8,128)(2,1)} %param.3), channel_id=1, replica_groups=mesh['dp'=16,'rep'=2] {'rep'}, dimensions={0}, use_global_device_ids=true | all-gather | bytes 786432 | tf_op jit(solution)/shard_map/all_gather | solution.py:88
  58.9 30.3 %all-gather.7.cloned.1.call-done = bf16[1024,2048]{1,0:T(8,128)(2,1)} async-done(((bf16[64,2048]{1,0:T(8,128)(2,1)}), bf16[1024,2048]{1,0:T(8,128)(2,1)}) %all-gather.7.cloned.1.call-update) | async-done | bytes 4194320 | tf_op jit(solution)/shard_map/all_gather | solution.py:91
  89.2 1.4 multiply_reduce_fusion.7
  90.7 1.5 multiply_reduce_fusion.6
  92.2 1.3 multiply_reduce_fusion.5
  93.5 1.3 multiply_reduce_fusion.4
  94.9 0.4 multiply_reduce_fusion.3
  95.3 0.3 multiply_reduce_fusion.2
  95.6 1.2 multiply_reduce_fusion.1
  96.9 1.5 multiply_reduce_fusion
  98.4 2.0 %fusion.197 = (f32[128]{0:T(128)S(1)}, f32[128,1024]{1,0:T(8,128)S(1)}) fusion(f32[128,1024]{1,0:T(8,128)S(1)} %get-tuple-element.60, bf16[1024,2048]{1,0:T(8,128)(2,1)S(1)} %copy-done.1, bf16[128,2048]{1,0:T(8,128)(2,1)} %copy-done.8), kind=kOutput, calls=%fused_computation.231 | convolution fusion | flops 268828544 | bytes 3408384 | tf_op jit(solution)/shard_map/dot_general | solution.py:21
  102.7 1.9 %all-gather.3 = f32[2,9,128]{2,1,0:T(8,128)S(1)} all-gather(f32[1,9,128]{2,1,0:T(8,128)S(1)} %bitcast.79), channel_id=3, replica_groups=mesh['dp'=16,'rep'=2] {'rep'}, dimensions={0}, use_global_device_ids=true | all-gather | bytes 13824 | tf_op jit(solution)/shard_map/all_gather | solution.py:11
  104.6 1.8 all-gather.2
  106.5 2.2 %fusion.53 = (f32[128,1024]{1,0:T(8,128)S(1)}, f32[128,1024]{1,0:T(8,128)S(1)}, bf16[128,1024]{1,0:T(8,128)(2,1)S(1)}, f32[128,1024]{1,0:T(8,128)S(1)}) fusion(f32[128,1024]{1,0:T(8,128)S(1)} %get-tuple-element.50, f32[128]{0:T(128)S(1)} %get-tuple-element.38, s32[1024]{0:T(1024)S(1)} %fusion.177, s32[128]{0:T(128)S(1)} %all-reduce, ...), kind=kLoop, calls=%fused_computation.68 | loop fusion | flops 4718592 | bytes 5513216 | tf_op jit(solution)/shard_map/add | solution.py:50
  108.9 0.3 fusion.121
  109.6 0.4 fusion.119
  110.0 0.4 fusion.123
  110.4 0.4 fusion.95
  111.1 0.5 fusion.130
  111.7 0.6 fusion.25
  112.2 1.3 concatenate.6
  113.5 40.8 %all_gather.38 = f32[9,2048]{1,0:T(8,128)S(1)} all-gather(f32[9,128]{1,0:T(8,128)S(1)} %fusion.165), channel_id=1, replica_groups=mesh['dp'=16,'rep'=2] {'dp'}, dimensions={1}, use_global_device_ids=true | all-gather | bytes 78336 | tf_op jit(solution)/shard_map/all_gather | solution.py:110
  154.4 14.2 %all-gather.9.cloned.1.call-done = bf16[2048,2048]{1,0:T(8,128)(2,1)} async-done(((bf16[64,2048]{1,0:T(8,128)(2,1)}), bf16[2048,2048]{1,0:T(8,128)(2,1)}) %all-gather.9.cloned.1.call-update) | async-done | bytes 8388624 | tf_op jit(solution)/shard_map/all_gather | solution.py:84
  168.6 1.5 fusion.93
  170.1 1.7 convolution_add_fusion.6
  171.8 1.4 convolution_add_fusion.5
  173.2 1.4 convolution_add_fusion.4
  174.7 1.4 convolution_add_fusion.3
  176.1 1.3 convolution_add_fusion.2
  177.4 0.4 convolution_add_fusion.1
  177.9 0.8 convolution_add_fusion
  178.7 2.0 %fusion.70 = (f32[64,2048]{1,0:T(8,128)S(1)}, f32[64,2048]{1,0:T(8,128)S(1)}, f32[64,2048]{1,0:T(8,128)S(1)}, f32[64,2048]{1,0:T(8,128)S(1)}) fusion(f32[64,2048]{1,0:T(8,128)S(1)} %convolution_add_fusion.5, f32[2048]{0:T(1024)S(1)} %bitcast.84, s32[2048]{0:T(1024)S(1)} %all-reduce.1, s32[64]{0:T(128)S(1)} %iota_add_fusion, f32[2048]{0:T(1024)S(1)} %bitcast.77, ...), kind=kOutput, calls=%fused_computation.85 | convolution fusion | flops 273285120 | bytes 9634304 | tf_op jit(solution)/shard_map/dot_general | solution.py:21
  180.7 0.4 fusion.85
  181.0 0.4 fusion.79
  181.4 0.5 fusion.82
  181.9 0.5 fusion.88
  182.3 0.4 fusion.76
  183.0 0.5 fusion.91
  183.5 0.5 fusion.22
  184.1 0.8 fusion
  184.9 0.9 concatenate.7
  (47 shorter events, 3.7 us)
Async XLA Ops:
  7.2 82.1 %all-gather.7.cloned.1.call-start = ((), (), s32[]{:S(2)}) async-start(), calls=%async_computation.1 | async-start | bytes 4456448 | tf_op jit(solution)/shard_map/all_gather | solution.py:91
  7.9 160.7 %all-gather.9.cloned.1.call-start = ((), (), s32[]{:S(2)}) async-start(), calls=%async_computation.3 | async-start | bytes 8650752 | tf_op jit(solution)/shard_map/all_gather | solution.py:84
  8.6 177.2 %reduce-scatter.2.cloned.1.call-start = ((), (), s32[]{:S(2)}) async-start(), calls=%async_computation.2 | async-start | bytes 1572864 | tf_op jit(solution)/shard_map/reduce_scatter | solution.py:109
  58.9 36.8 %copy-start.8 = (bf16[128,2048]{1,0:T(8,128)(2,1)}, bf16[128,2048]{1,0:T(8,128)(2,1)S(1)}, u32[]{:S(2)}) copy-start(bf16[128,2048]{1,0:T(8,128)(2,1)S(1)} %all_gather.30) | copy-start | bytes 1572868
  89.2 5.7 %copy-start.1 = (bf16[1024,2048]{1,0:T(8,128)(2,1)S(1)}, bf16[1024,2048]{1,0:T(8,128)(2,1)}, u32[]{:S(2)}) copy-start(bf16[1024,2048]{1,0:T(8,128)(2,1)} %all-gather.7.cloned.1.call-done) | copy-start | bytes 12582916
  90.7 10.0 %copy-start.3 = (f32[128,1024]{1,0:T(8,128)}, f32[128,1024]{1,0:T(8,128)S(1)}, u32[]{:S(2)}) copy-start(f32[128,1024]{1,0:T(8,128)S(1)} %get-tuple-element.46) | copy-start | bytes 1572868
  98.4 4.0 %copy-start.5 = (f32[128,1024]{1,0:T(8,128)}, f32[128,1024]{1,0:T(8,128)S(1)}, u32[]{:S(2)}) copy-start(f32[128,1024]{1,0:T(8,128)S(1)} %get-tuple-element.60) | copy-start | bytes 1572868
  100.4 2.2 %copy-start.6 = (f32[128,1024]{1,0:T(8,128)}, f32[128,1024]{1,0:T(8,128)S(1)}, u32[]{:S(2)}) copy-start(f32[128,1024]{1,0:T(8,128)S(1)} %get-tuple-element.62) | copy-start | bytes 1572868
  102.7 6.0 %copy-start.2 = (bf16[1024,2048]{1,0:T(8,128)(2,1)S(1)}, bf16[1024,2048]{1,0:T(8,128)(2,1)}, u32[]{:S(2)}) copy-start(bf16[1024,2048]{1,0:T(8,128)(2,1)} %all-gather.7.cloned.1.call-done) | copy-start | bytes 12582916
  108.7 2.4 %copy-start.4 = (f32[128,1024]{1,0:T(8,128)S(1)}, f32[128,1024]{1,0:T(8,128)}, u32[]{:S(2)}) copy-start(f32[128,1024]{1,0:T(8,128)} %copy-done.3) | copy-start | bytes 1572868
  109.6 2.1 %copy-start.7 = (f32[128,1024]{1,0:T(8,128)S(1)}, f32[128,1024]{1,0:T(8,128)}, u32[]{:S(2)}) copy-start(f32[128,1024]{1,0:T(8,128)} %copy-done.6) | copy-start | bytes 1572868
  111.1 57.5 %copy-start.9 = (bf16[64,2048]{1,0:T(8,128)(2,1)S(1)}, bf16[64,2048]{1,0:T(8,128)(2,1)}, u32[]{:S(2)}) copy-start(bf16[64,2048]{1,0:T(8,128)(2,1)} %param.4) | copy-start | bytes 786436
  168.6 8.8 %copy-start = (bf16[2048,2048]{1,0:T(8,128)(2,1)S(1)}, bf16[2048,2048]{1,0:T(8,128)(2,1)}, u32[]{:S(2)}) copy-start(bf16[2048,2048]{1,0:T(8,128)(2,1)} %all-gather.9.cloned.1.call-done) | copy-start | bytes 25165828
Sparse Core Ops, SparseCore 0:
  10.7 78.4 all-gather.6
  92.1 76.4 all-gather.8
  171.4 7.1 reduce-scatter.1
where the time goes:
time: 193 us; the launch traced here: 192 us
  blocking collectives  91.1 us (47%)
  waiting for transfers between devices  46 us (24%)
  matrix products  30.8 us (16%)
  between operations  14.7 us (8%)
  local copies, waits for them, and re-layouts  5.31 us (3%)
  other arithmetic  4.33 us (2%)
    unnamed x2, blocking collectives  44.2 us
    all_gather x1, blocking collectives, on_device(): all_totals = lax.all_gather(totals, 'dp', axis=1, tiled=True)  40.8 us
    all_gather x1, waiting for transfers between devices, on_device(): partner_docs = lax.all_gather(documents, 'dp', axis=0, tiled=True)  30.3 us
    dot_general x18, matrix products, contract(): lax.dot_general(first_op, second_op, (((1,), (1,)), ((), ())), preferred_...  23.2 us
    all_gather x1, waiting for transfers between devices, on_device(): lax.all_gather(queries, ('dp', 'rep'), axis=0, tiled=True)  14.2 us
    dot_general x18, matrix products, spread(): jnp.dot(bands[nested], block_part, preferred_element_type=jnp.float32)  7.64 us
  transfers between devices with their start and end apart: 3, of which 2 were waited for; matrix products, arithmetic and copies ran while one was open for 21% of the time, Pallas kernels for 0%

commit v1 on v0

--- a/solution.py
+++ b/solution.py
@@ -5,6 +5,17 @@
 
 WIDTHS = 9
 logit_gain = 3.0
+
+
+def turned_line(x, mesh_axis, d):
+    n_dev = lax.axis_size(mesh_axis)
+    route = [(i, (i + 1) % n_dev) for i in range(n_dev)]
+    blocks = [x]
+    for hop in range(1, n_dev):
+        blocks = [lax.ppermute(blocks[0], mesh_axis, route), *blocks]
+    out = jnp.concatenate(blocks, axis=d)
+    turn = (lax.axis_index(mesh_axis) + 1) * blocks[-1].shape[d]
+    return jnp.roll(out, turn, axis=d)
 
 
 def merged(x, axis, combine):
@@ -107,7 +118,7 @@
     )
     partial_queries = spread(bands, partner_docs, uppers)
     grad_queries = lax.psum_scatter(partial_queries, "rep", scatter_dimension=0, tiled=True)
-    all_totals = lax.all_gather(totals, "dp", axis=1, tiled=True)
+    all_totals = turned_line(totals, "dp", 1)
     own_ids = (dp_index * rep_count + rep_index) * own_rows + jnp.arange(own_rows, dtype=jnp.int32)
     own_target = (own_ids[:, None] == every_partner[None, :]).astype(jnp.float32)
     own_logits = scores(documents, every_rows)

time: 193 us -> 280 us (1.45)
  waiting for transfers between devices: 46 us -> 170 us
  blocking collectives: 91.1 us -> 50.4 us
  starting transfers between devices: 0.11 us -> 3.93 us
    ppermute x0 -> x15, waiting for transfers between devices: none -> 91 us  [turned_line(): blocks = [lax.ppermute(blocks[0], mesh_axis, route), *blocks]]
    all_gather x1, waiting for transfers between devices: 30.3 us -> 77.9 us  [on_device(): partner_docs = lax.all_gather(documents, 'dp', axis=0, tiled=True)]
    all_gather x1 -> x0, blocking collectives: 40.8 us -> none  [on_device(): all_totals = lax.all_gather(totals, 'dp', axis=1, tiled=True)]
    all_gather x1, waiting for transfers between devices: 14.2 us -> 0.02 us  [on_device(): lax.all_gather(queries, ('dp', 'rep'), axis=0, tiled=True)]
    ppermute x0 -> x15, starting transfers between devices: none -> 3.81 us  [turned_line(): blocks = [lax.ppermute(blocks[0], mesh_axis, route), *blocks]]
  transfers between devices with their start and end apart: 3 -> 18, of which waited for: 2 -> 15; matrix products, arithmetic and copies ran while one was open for 21% -> 14% of each run, Pallas kernels for 0% -> 0%
where the time goes in v1:
time: 280 us; the launch traced here: 279 us
  waiting for transfers between devices  170 us (61%)
  blocking collectives  50.4 us (18%)
  matrix products  31.4 us (11%)
  between operations  14.9 us (5%)
  other arithmetic  4.39 us (2%)
  starting transfers between devices  3.93 us (1%)
  local copies, waits for them, and re-layouts  3.73 us (1%)
    ppermute x15, waiting for transfers between devices, turned_line(): blocks = [lax.ppermute(blocks[0], mesh_axis, route), *blocks]  91 us
    all_gather x1, waiting for transfers between devices, on_device(): partner_docs = lax.all_gather(documents, 'dp', axis=0, tiled=True)  77.9 us
    unnamed x2, blocking collectives  44.3 us
    dot_general x18, matrix products, contract(): lax.dot_general(first_op, second_op, (((1,), (1,)), ((), ())), preferred_...  23.6 us
    dot_general x18, matrix products, spread(): jnp.dot(bands[nested], block_part, preferred_element_type=jnp.float32)  7.8 us
  transfers between devices with their start and end apart: 18, of which 15 were waited for; matrix products, arithmetic and copies ran while one was open for 14% of the time, Pallas kernels for 0%

profile of v1, /device:TPU:0, one launch (start us, length us, event | category | flops | bytes accessed | tf_op | source)
XLA Modules:
  0.0 279.1 jit_solution(6944885233646773451)
XLA Ops:
  7.2 0.7 all-gather.7.cloned.1.call-update
  7.9 0.7 all-gather.9.cloned.1.call-update
  8.7 2.5 all_gather.27
  11.2 77.9 %all-gather.7.cloned.1.call-done = bf16[1024,2048]{1,0:T(8,128)(2,1)} async-done(((bf16[64,2048]{1,0:T(8,128)(2,1)}), bf16[1024,2048]{1,0:T(8,128)(2,1)}) %all-gather.7.cloned.1.call-update) | async-done | bytes 4194320 | tf_op jit(solution)/shard_map/all_gather | solution.py:102
  89.1 1.4 multiply_reduce_fusion.7
  90.5 1.5 multiply_reduce_fusion.6
  92.1 1.4 multiply_reduce_fusion.5
  93.4 1.4 multiply_reduce_fusion.4
  95.5 1.2 multiply_reduce_fusion.1
  96.8 1.5 multiply_reduce_fusion
  98.3 2.1 fusion.192
  102.6 1.8 all-gather.3
  104.4 1.8 all-gather.2
  106.2 1.5 collective-permute-start
  107.7 5.9 %collective-permute-done = f32[9,128]{1,0:T(8,128)S(1)} collective-permute-done((f32[9,128]{1,0:T(8,128)S(1)}, f32[9,128]{1,0:T(8,128)S(1)}, u32[]{:S(2)}, u32[]{:S(2)}) %collective-permute-start) | collective-permute-done | bytes 4640 | tf_op jit(solution)/shard_map/ppermute | solution.py:15
  113.6 7.3 %collective-permute-done.1 = f32[9,128]{1,0:T(8,128)S(1)} collective-permute-done((f32[9,128]{1,0:T(8,128)S(1)}, f32[9,128]{1,0:T(8,128)S(1)}, u32[]{:S(2)}, u32[]{:S(2)}) %collective-permute-start.1) | collective-permute-done | bytes 4640 | tf_op jit(solution)/shard_map/ppermute | solution.py:15
  121.0 7.4 %collective-permute-done.2 = f32[9,128]{1,0:T(8,128)S(1)} collective-permute-done((f32[9,128]{1,0:T(8,128)S(1)}, f32[9,128]{1,0:T(8,128)S(1)}, u32[]{:S(2)}, u32[]{:S(2)}) %collective-permute-start.2) | collective-permute-done | bytes 4640 | tf_op jit(solution)/shard_map/ppermute | solution.py:15
  128.4 0.6 dynamic-slice
  130.2 1.8 all-reduce
  132.0 42.5 %all-reduce.1 = s32[2048]{0:T(1024)S(1)} all-reduce(s32[2048]{0:T(1024)S(1)} %dynamic-update-slice.1), channel_id=1, replica_groups=mesh['dp'=16,'rep'=2] {'dp','rep'}, use_global_device_ids=true, to_apply=%add.1 | all-reduce | flops 2048 | bytes 16384
  174.5 2.3 collective-permute-start.4
  176.8 5.0 %collective-permute-done.4 = f32[9,128]{1,0:T(8,128)S(1)} collective-permute-done((f32[9,128]{1,0:T(8,128)S(1)}, f32[9,128]{1,0:T(8,128)S(1)}, u32[]{:S(2)}, u32[]{:S(2)}) %collective-permute-start.4) | collective-permute-done | bytes 4640 | tf_op jit(solution)/shard_map/ppermute | solution.py:15
  181.8 2.2 fusion.41
  184.0 5.0 %collective-permute-done.5 = f32[9,128]{1,0:T(8,128)S(1)} collective-permute-done((f32[9,128]{1,0:T(8,128)S(1)}, f32[9,128]{1,0:T(8,128)S(1)}, u32[]{:S(2)}, u32[]{:S(2)}) %collective-permute-start.5) | collective-permute-done | bytes 4640 | tf_op jit(solution)/shard_map/ppermute | solution.py:15
  189.0 0.6 fusion.13
  189.6 6.7 %collective-permute-done.6 = f32[9,128]{1,0:T(8,128)S(1)} collective-permute-done((f32[9,128]{1,0:T(8,128)S(1)}, f32[9,128]{1,0:T(8,128)S(1)}, u32[]{:S(2)}, u32[]{:S(2)}) %collective-permute-start.6) | collective-permute-done | bytes 4640 | tf_op jit(solution)/shard_map/ppermute | solution.py:15
  196.3 0.5 fusion.124
  196.8 6.7 %collective-permute-done.7 = f32[9,128]{1,0:T(8,128)S(1)} collective-permute-done((f32[9,128]{1,0:T(8,128)S(1)}, f32[9,128]{1,0:T(8,128)S(1)}, u32[]{:S(2)}, u32[]{:S(2)}) %collective-permute-start.7) | collective-permute-done | bytes 4640 | tf_op jit(solution)/shard_map/ppermute | solution.py:15
  203.8 6.9 %collective-permute-done.8 = f32[9,128]{1,0:T(8,128)S(1)} collective-permute-done((f32[9,128]{1,0:T(8,128)S(1)}, f32[9,128]{1,0:T(8,128)S(1)}, u32[]{:S(2)}, u32[]{:S(2)}) %collective-permute-start.8) | collective-permute-done | bytes 4640 | tf_op jit(solution)/shard_map/ppermute | solution.py:15
  211.1 6.9 %collective-permute-done.9 = f32[9,128]{1,0:T(8,128)S(1)} collective-permute-done((f32[9,128]{1,0:T(8,128)S(1)}, f32[9,128]{1,0:T(8,128)S(1)}, u32[]{:S(2)}, u32[]{:S(2)}) %collective-permute-start.9) | collective-permute-done | bytes 4640 | tf_op jit(solution)/shard_map/ppermute | solution.py:15
  218.4 6.8 %collective-permute-done.10 = f32[9,128]{1,0:T(8,128)S(1)} collective-permute-done((f32[9,128]{1,0:T(8,128)S(1)}, f32[9,128]{1,0:T(8,128)S(1)}, u32[]{:S(2)}, u32[]{:S(2)}) %collective-permute-start.10) | collective-permute-done | bytes 4640 | tf_op jit(solution)/shard_map/ppermute | solution.py:15
  225.7 6.8 %collective-permute-done.11 = f32[9,128]{1,0:T(8,128)S(1)} collective-permute-done((f32[9,128]{1,0:T(8,128)S(1)}, f32[9,128]{1,0:T(8,128)S(1)}, u32[]{:S(2)}, u32[]{:S(2)}) %collective-permute-start.11) | collective-permute-done | bytes 4640 | tf_op jit(solution)/shard_map/ppermute | solution.py:15
  232.8 6.9 %collective-permute-done.12 = f32[9,128]{1,0:T(8,128)S(1)} collective-permute-done((f32[9,128]{1,0:T(8,128)S(1)}, f32[9,128]{1,0:T(8,128)S(1)}, u32[]{:S(2)}, u32[]{:S(2)}) %collective-permute-start.12) | collective-permute-done | bytes 4640 | tf_op jit(solution)/shard_map/ppermute | solution.py:15
  240.1 6.9 %collective-permute-done.13 = f32[9,128]{1,0:T(8,128)S(1)} collective-permute-done((f32[9,128]{1,0:T(8,128)S(1)}, f32[9,128]{1,0:T(8,128)S(1)}, u32[]{:S(2)}, u32[]{:S(2)}) %collective-permute-start.13) | collective-permute-done | bytes 4640 | tf_op jit(solution)/shard_map/ppermute | solution.py:15
  247.3 1.3 concatenate.12
  248.6 5.7 %collective-permute-done.14 = f32[9,128]{1,0:T(8,128)S(1)} collective-permute-done((f32[9,128]{1,0:T(8,128)S(1)}, f32[9,128]{1,0:T(8,128)S(1)}, u32[]{:S(2)}, u32[]{:S(2)}) %collective-permute-start.14) | collective-permute-done | bytes 4640 | tf_op jit(solution)/shard_map/ppermute | solution.py:15
  254.8 1.5 fusion.82
  256.4 2.1 convolution_add_fusion.6
  258.5 1.4 convolution_add_fusion.5
  259.9 1.4 convolution_add_fusion.4
  261.3 1.4 convolution_add_fusion.3
  262.7 1.3 convolution_add_fusion.2
  264.5 0.8 convolution_add_fusion
  265.3 2.0 fusion.59
  268.0 0.5 fusion.71
  270.1 0.7 fusion.10
  270.8 0.9 fusion
  271.7 0.9 concatenate.14
  (112 shorter events, 9.2 us)
Async XLA Ops:
  7.2 81.9 %all-gather.7.cloned.1.call-start = ((), (), s32[]{:S(2)}) async-start(), calls=%async_computation.1 | async-start | bytes 4456448 | tf_op jit(solution)/shard_map/all_gather | solution.py:102
  7.9 246.9 %all-gather.9.cloned.1.call-start = ((), (), s32[]{:S(2)}) async-start(), calls=%async_computation.3 | async-start | bytes 8650752 | tf_op jit(solution)/shard_map/all_gather | solution.py:95
  8.6 264.0 %reduce-scatter.2.cloned.1.call-start = ((), (), s32[]{:S(2)}) async-start(), calls=%async_computation.2 | async-start | bytes 1572864 | tf_op jit(solution)/shard_map/reduce_scatter | solution.py:120
  11.2 84.3 %copy-start.8 = (bf16[128,2048]{1,0:T(8,128)(2,1)}, bf16[128,2048]{1,0:T(8,128)(2,1)S(1)}, u32[]{:S(2)}) copy-start(bf16[128,2048]{1,0:T(8,128)(2,1)S(1)} %all_gather.27) | copy-start | bytes 1572868
  89.1 5.7 %copy-start.1 = (bf16[1024,2048]{1,0:T(8,128)(2,1)S(1)}, bf16[1024,2048]{1,0:T(8,128)(2,1)}, u32[]{:S(2)}) copy-start(bf16[1024,2048]{1,0:T(8,128)(2,1)} %all-gather.7.cloned.1.call-done) | copy-start | bytes 12582916
  90.5 10.1 %copy-start.3 = (f32[128,1024]{1,0:T(8,128)}, f32[128,1024]{1,0:T(8,128)S(1)}, u32[]{:S(2)}) copy-start(f32[128,1024]{1,0:T(8,128)S(1)} %get-tuple-element.46) | copy-start | bytes 1572868
  98.2 4.0 %copy-start.5 = (f32[128,1024]{1,0:T(8,128)}, f32[128,1024]{1,0:T(8,128)S(1)}, u32[]{:S(2)}) copy-start(f32[128,1024]{1,0:T(8,128)S(1)} %get-tuple-element.60) | copy-start | bytes 1572868
  98.2 30.2 %copy-start.11 = (u32[32]{0:T(128)S(1)}, u32[32]{0:T(128)}, u32[]{:S(2)}) copy-start(u32[32]{0:T(128)} %constant.109) | copy-start | bytes 388
  98.3 31.4 %copy-start.10 = (s32[64]{0:T(128)S(1)}, s32[64]{0:T(128)}, u32[]{:S(2)}) copy-start(s32[64]{0:T(128)} %param.5) | copy-start | bytes 772
  100.3 2.2 copy-start.6
  106.2 7.4 %collective-permute-start = (f32[9,128]{1,0:T(8,128)S(1)}, f32[9,128]{1,0:T(8,128)S(1)}, u32[]{:S(2)}, u32[]{:S(2)}) collective-permute-start(f32[9,128]{1,0:T(8,128)S(1)} %fusion.159), channel_id=1, source_target_pairs={{0,2},{2,4},{4,6},{6,8},{8,10},{10,12},{12,14},{14,16},{16,18},{18... | collective-permute-start | bytes 13832 | tf_op jit(solution)/shard_map/ppermute | solution.py:15
  113.6 7.4 %collective-permute-start.1 = (f32[9,128]{1,0:T(8,128)S(1)}, f32[9,128]{1,0:T(8,128)S(1)}, u32[]{:S(2)}, u32[]{:S(2)}) collective-permute-start(f32[9,128]{1,0:T(8,128)S(1)} %collective-permute-done), channel_id=1, source_target_pairs={{0,2},{2,4},{4,6},{6,8},{8,10},{10,12},{12,14},{14,16},{16,18},{18... | collective-permute-start | bytes 13832 | tf_op jit(solution)/shard_map/ppermute | solution.py:15
  121.0 7.5 %collective-permute-start.2 = (f32[9,128]{1,0:T(8,128)S(1)}, f32[9,128]{1,0:T(8,128)S(1)}, u32[]{:S(2)}, u32[]{:S(2)}) collective-permute-start(f32[9,128]{1,0:T(8,128)S(1)} %collective-permute-done.1), channel_id=1, source_target_pairs={{0,2},{2,4},{4,6},{6,8},{8,10},{10,12},{12,14},{14,16},{16,18},{18... | collective-permute-start | bytes 13832 | tf_op jit(solution)/shard_map/ppermute | solution.py:15
  128.4 46.1 %collective-permute-start.3 = (f32[9,128]{1,0:T(8,128)S(1)}, f32[9,128]{1,0:T(8,128)S(1)}, u32[]{:S(2)}, u32[]{:S(2)}) collective-permute-start(f32[9,128]{1,0:T(8,128)S(1)} %collective-permute-done.2), channel_id=1, source_target_pairs={{0,2},{2,4},{4,6},{6,8},{8,10},{10,12},{12,14},{14,16},{16,18},{18... | collective-permute-start | bytes 13832 | tf_op jit(solution)/shard_map/ppermute | solution.py:15
  174.5 14.6 %copy-start.2 = (bf16[1024,2048]{1,0:T(8,128)(2,1)S(1)}, bf16[1024,2048]{1,0:T(8,128)(2,1)}, u32[]{:S(2)}) copy-start(bf16[1024,2048]{1,0:T(8,128)(2,1)} %all-gather.7.cloned.1.call-done) | copy-start | bytes 12582916
  174.5 14.6 %copy-start.7 = (f32[128,1024]{1,0:T(8,128)S(1)}, f32[128,1024]{1,0:T(8,128)}, u32[]{:S(2)}) copy-start(f32[128,1024]{1,0:T(8,128)} %copy-done.6) | copy-start | bytes 1572868
  174.5 7.3 %collective-permute-start.4 = (f32[9,128]{1,0:T(8,128)S(1)}, f32[9,128]{1,0:T(8,128)S(1)}, u32[]{:S(2)}, u32[]{:S(2)}) collective-permute-start(f32[9,128]{1,0:T(8,128)S(1)} %collective-permute-done.3), channel_id=1, source_target_pairs={{0,2},{2,4},{4,6},{6,8},{8,10},{10,12},{12,14},{14,16},{16,18},{18... | collective-permute-start | bytes 13832 | tf_op jit(solution)/shard_map/ppermute | solution.py:15
  181.8 7.2 %collective-permute-start.5 = (f32[9,128]{1,0:T(8,128)S(1)}, f32[9,128]{1,0:T(8,128)S(1)}, u32[]{:S(2)}, u32[]{:S(2)}) collective-permute-start(f32[9,128]{1,0:T(8,128)S(1)} %collective-permute-done.4), channel_id=1, source_target_pairs={{0,2},{2,4},{4,6},{6,8},{8,10},{10,12},{12,14},{14,16},{16,18},{18... | collective-permute-start | bytes 13832 | tf_op jit(solution)/shard_map/ppermute | solution.py:15
  181.8 14.5 %copy-start.4 = (f32[128,1024]{1,0:T(8,128)S(1)}, f32[128,1024]{1,0:T(8,128)}, u32[]{:S(2)}) copy-start(f32[128,1024]{1,0:T(8,128)} %copy-done.3) | copy-start | bytes 1572868
  189.0 7.2 %collective-permute-start.6 = (f32[9,128]{1,0:T(8,128)S(1)}, f32[9,128]{1,0:T(8,128)S(1)}, u32[]{:S(2)}, u32[]{:S(2)}) collective-permute-start(f32[9,128]{1,0:T(8,128)S(1)} %collective-permute-done.5), channel_id=1, source_target_pairs={{0,2},{2,4},{4,6},{6,8},{8,10},{10,12},{12,14},{14,16},{16,18},{18... | collective-permute-start | bytes 13832 | tf_op jit(solution)/shard_map/ppermute | solution.py:15
  196.3 7.2 %collective-permute-start.7 = (f32[9,128]{1,0:T(8,128)S(1)}, f32[9,128]{1,0:T(8,128)S(1)}, u32[]{:S(2)}, u32[]{:S(2)}) collective-permute-start(f32[9,128]{1,0:T(8,128)S(1)} %collective-permute-done.6), channel_id=1, source_target_pairs={{0,2},{2,4},{4,6},{6,8},{8,10},{10,12},{12,14},{14,16},{16,18},{18... | collective-permute-start | bytes 13832 | tf_op jit(solution)/shard_map/ppermute | solution.py:15
  203.5 7.2 %collective-permute-start.8 = (f32[9,128]{1,0:T(8,128)S(1)}, f32[9,128]{1,0:T(8,128)S(1)}, u32[]{:S(2)}, u32[]{:S(2)}) collective-permute-start(f32[9,128]{1,0:T(8,128)S(1)} %collective-permute-done.7), channel_id=1, source_target_pairs={{0,2},{2,4},{4,6},{6,8},{8,10},{10,12},{12,14},{14,16},{16,18},{18... | collective-permute-start | bytes 13832 | tf_op jit(solution)/shard_map/ppermute | solution.py:15
  210.8 7.2 %collective-permute-start.9 = (f32[9,128]{1,0:T(8,128)S(1)}, f32[9,128]{1,0:T(8,128)S(1)}, u32[]{:S(2)}, u32[]{:S(2)}) collective-permute-start(f32[9,128]{1,0:T(8,128)S(1)} %collective-permute-done.8), channel_id=1, source_target_pairs={{0,2},{2,4},{4,6},{6,8},{8,10},{10,12},{12,14},{14,16},{16,18},{18... | collective-permute-start | bytes 13832 | tf_op jit(solution)/shard_map/ppermute | solution.py:15
  218.0 7.2 %collective-permute-start.10 = (f32[9,128]{1,0:T(8,128)S(1)}, f32[9,128]{1,0:T(8,128)S(1)}, u32[]{:S(2)}, u32[]{:S(2)}) collective-permute-start(f32[9,128]{1,0:T(8,128)S(1)} %collective-permute-done.9), channel_id=1, source_target_pairs={{0,2},{2,4},{4,6},{6,8},{8,10},{10,12},{12,14},{14,16},{16,18},{18... | collective-permute-start | bytes 13832 | tf_op jit(solution)/shard_map/ppermute | solution.py:15
  218.4 36.4 %copy-start.9 = (bf16[64,2048]{1,0:T(8,128)(2,1)S(1)}, bf16[64,2048]{1,0:T(8,128)(2,1)}, u32[]{:S(2)}) copy-start(bf16[64,2048]{1,0:T(8,128)(2,1)} %param.4) | copy-start | bytes 786436
  225.3 7.2 %collective-permute-start.11 = (f32[9,128]{1,0:T(8,128)S(1)}, f32[9,128]{1,0:T(8,128)S(1)}, u32[]{:S(2)}, u32[]{:S(2)}) collective-permute-start(f32[9,128]{1,0:T(8,128)S(1)} %collective-permute-done.10), channel_id=1, source_target_pairs={{0,2},{2,4},{4,6},{6,8},{8,10},{10,12},{12,14},{14,16},{16,18},{18... | collective-permute-start | bytes 13832 | tf_op jit(solution)/shard_map/ppermute | solution.py:15
  232.5 7.2 %collective-permute-start.12 = (f32[9,128]{1,0:T(8,128)S(1)}, f32[9,128]{1,0:T(8,128)S(1)}, u32[]{:S(2)}, u32[]{:S(2)}) collective-permute-start(f32[9,128]{1,0:T(8,128)S(1)} %collective-permute-done.11), channel_id=1, source_target_pairs={{0,2},{2,4},{4,6},{6,8},{8,10},{10,12},{12,14},{14,16},{16,18},{18... | collective-permute-start | bytes 13832 | tf_op jit(solution)/shard_map/ppermute | solution.py:15
  239.7 7.2 %collective-permute-start.13 = (f32[9,128]{1,0:T(8,128)S(1)}, f32[9,128]{1,0:T(8,128)S(1)}, u32[]{:S(2)}, u32[]{:S(2)}) collective-permute-start(f32[9,128]{1,0:T(8,128)S(1)} %collective-permute-done.12), channel_id=1, source_target_pairs={{0,2},{2,4},{4,6},{6,8},{8,10},{10,12},{12,14},{14,16},{16,18},{18... | collective-permute-start | bytes 13832 | tf_op jit(solution)/shard_map/ppermute | solution.py:15
  247.0 7.2 %collective-permute-start.14 = (f32[9,128]{1,0:T(8,128)S(1)}, f32[9,128]{1,0:T(8,128)S(1)}, u32[]{:S(2)}, u32[]{:S(2)}) collective-permute-start(f32[9,128]{1,0:T(8,128)S(1)} %collective-permute-done.13), channel_id=1, source_target_pairs={{0,2},{2,4},{4,6},{6,8},{8,10},{10,12},{12,14},{14,16},{16,18},{18... | collective-permute-start | bytes 13832 | tf_op jit(solution)/shard_map/ppermute | solution.py:15
  254.8 9.3 %copy-start = (bf16[2048,2048]{1,0:T(8,128)(2,1)S(1)}, bf16[2048,2048]{1,0:T(8,128)(2,1)}, u32[]{:S(2)}) copy-start(bf16[2048,2048]{1,0:T(8,128)(2,1)} %all-gather.9.cloned.1.call-done) | copy-start | bytes 25165828
Sparse Core Ops, SparseCore 0:
  10.7 78.3 all-gather.6
  91.9 76.7 all-gather.8
  248.7 9.7 reduce-scatter.1
